TPU v7x, 128 devices: a whole 4x4x4 slice. The times are simulated.
128 devices in a mesh: ctx: 16 (over y, x), tp: 8 (over z, core).
Axes of the slice: x: 4, y: 4, z: 4, core: 2. Of those that a mesh axis runs over, the one named last changes fastest.
Arguments:
- hidden: bfloat16 [8, 8192], P(None, 'ctx'), may hold values from -4.8 to 4.8, as said below
- norm_gains: bfloat16 [4, 8192], P(None, 'ctx'), may hold values from 0.5 to 1.5
- w_query: bfloat16 [4, 8192, 8192], P(None, 'ctx', 'tp'), may hold values from -0.0625 to 0.0625
- w_key: bfloat16 [4, 8192, 1024], P(None, 'ctx', 'tp'), may hold values from -0.125 to 0.125
- w_value: bfloat16 [4, 8192, 1024], P(None, 'ctx', 'tp'), may hold values from -0.125 to 0.125
- w_out: bfloat16 [4, 8192, 8192], P(None, 'tp', 'ctx'), may hold values from -0.0625 to 0.0625
- key_cache: bfloat16 [4, 8, 8, 2048, 128], P(None, None, 'tp', 'ctx'), may hold values from -9 to 9
- value_cache: bfloat16 [4, 8, 8, 2048, 128], P(None, None, 'tp', 'ctx'), may hold values from -6 to 6
- lengths: int32 [8], replicated, may hold values from 1 to 2048, 8200 in all
Outputs:
- updated: float32 [8, 8192], P(None, 'ctx')
Inputs may be any that keep to these rules, and one draw needn't show every extreme that they name: Each sequence has lengths[b] valid cache positions 0 .. lengths[b] - 1, between 1 and 2048; the longest sequence has exactly 2048; the new token sits at position lengths[b]. `hidden`: activations of order 0.2; in each block of 512 consecutive features one sequence, chosen at random, has entries four times larger.
All inputs are finite; a program needn't handle non-finite values.
Results may differ from a plain program's by a relative error of at most 0.02.
Values sent between devices are 32-bit elements.
A program may use at most 64 MiB of HBM per device.

v0:
```python
import functools
import math

import jax
import jax.numpy as jnp
from jax import lax
from jax.sharding import Mesh
from jax.sharding import PartitionSpec as P

D = 8192
CTX = ("ctx_0", "ctx_1")


mask_fill = -1e30
norm_eps = 1e-05
rope_base = 500000.0


def over_axes(shard, axes):
    return functools.reduce(lax.psum, axes, shard)


def one_axis_at_a_time(shard, axes):
    for axis in axes:
        shard = lax.pmax(shard, axis)
    return shard


def over_pieces(shard, axis):
    return lax.all_gather(shard, axis).sum(0)


def rotate(vectors, positions):
    width = vectors.shape[-1]
    half_width = width // 2
    exponents = jnp.arange(half_width, dtype=jnp.float32) * (2.0 / width)
    frequency = jnp.exp(-exponents * math.log(rope_base))
    angles = positions.astype(jnp.float32)[:, None] * frequency[None, :]
    cosine = jnp.cos(angles)[:, None, :]
    sine_part = jnp.sin(angles)[:, None, :]
    first_half = vectors[..., :half_width]
    second_half = vectors[..., half_width:]
    return jnp.concatenate(
        [
            first_half * cosine - second_half * sine_part,
            second_half * cosine + first_half * sine_part,
        ],
        axis=-1,
    )


def on_device(hidden, norm_gains, w_query, w_key, w_value, w_out, key_cache, value_cache, lengths):
    stream = hidden.astype(jnp.float32)
    seq_count = hidden.shape[0]
    head_width = key_cache.shape[4]
    location_total = key_cache.shape[3]
    kv_local = key_cache.shape[2]
    query_local = w_query.shape[2] // head_width
    group_size = query_local // kv_local
    logit_multiplier = 1.0 / math.sqrt(head_width)
    positions = lax.axis_index(CTX) * location_total + jnp.arange(location_total, dtype=jnp.int32)
    usable = (positions[None, :] < lengths[:, None])[:, None, None, :]
    for layer_idx in range(w_query.shape[0]):
        local_squares = jnp.sum(stream * stream, axis=1)
        scaled = (stream * norm_gains[layer_idx].astype(jnp.float32)).astype(jnp.bfloat16)
        query_part = jnp.dot(scaled, w_query[layer_idx], preferred_element_type=jnp.float32)
        key_part = jnp.dot(scaled, w_key[layer_idx], preferred_element_type=jnp.float32)
        value_part = jnp.dot(scaled, w_value[layer_idx], preferred_element_type=jnp.float32)
        squares = over_axes(local_squares, CTX)
        raw_query, raw_key, raw_value = (
            over_axes(query_part, CTX),
            over_axes(key_part, CTX),
            over_axes(value_part, CTX),
        )
        reciprocal_value = lax.rsqrt(squares / D + norm_eps)
        query = rotate(
            (raw_query * reciprocal_value[:, None]).reshape(seq_count, query_local, head_width),
            lengths,
        ).astype(jnp.bfloat16)
        fresh_lookup_vector = rotate(
            (raw_key * reciprocal_value[:, None]).reshape(seq_count, kv_local, head_width), lengths
        ).astype(jnp.bfloat16)
        new_value = (
            (raw_value * reciprocal_value[:, None])
            .reshape(seq_count, kv_local, head_width)
            .astype(jnp.bfloat16)
        )
        shared_head_sets = query.reshape(seq_count, kv_local, group_size, head_width)
        scores = (
            jnp.einsum(
                "bkgd,bksd->bkgs",
                shared_head_sets,
                key_cache[layer_idx],
                preferred_element_type=jnp.float32,
            )
            * logit_multiplier
        )
        masked = jnp.where(usable, scores, mask_fill)
        local_max = jnp.max(masked, axis=-1)
        attention_probabilities = jnp.where(usable, jnp.exp(masked - local_max[..., None]), 0.0)
        local_sum = jnp.sum(attention_probabilities, axis=-1)
        local_out = jnp.einsum(
            "bkgs,bksd->bkgd",
            attention_probabilities.astype(jnp.bfloat16),
            value_cache[layer_idx],
            preferred_element_type=jnp.float32,
        )
        largest = one_axis_at_a_time(local_max, CTX)
        factor = jnp.exp(local_max - largest)
        total_sum, total_out = (
            over_axes(local_sum * factor, CTX),
            over_axes(local_out * factor[..., None], CTX),
        )
        self_match_logit = (
            jnp.einsum(
                "uryj,urj->ury",
                shared_head_sets,
                fresh_lookup_vector,
                preferred_element_type=jnp.float32,
            )
            * logit_multiplier
        )
        row_top = jnp.maximum(largest, self_match_logit)
        carried = jnp.exp(largest - row_top)
        fresh = jnp.exp(self_match_logit - row_top)
        fresh_rounded = lax.optimization_barrier(fresh.astype(jnp.bfloat16)).astype(jnp.float32)
        numerator = (
            total_out * carried[..., None]
            + fresh_rounded[..., None] * new_value.astype(jnp.float32)[:, :, None, :]
        )
        denominator = total_sum * carried + fresh
        context = (
            (numerator / denominator[..., None])
            .reshape(seq_count, query_local * head_width)
            .astype(jnp.bfloat16)
        )
        head_part = jnp.dot(context, w_out[layer_idx], preferred_element_type=jnp.float32)
        stream = stream + over_pieces(head_part, "tp")
    return stream


def solution(mesh):
    finer = Mesh(mesh.devices.reshape(4, 4, mesh.shape["tp"]), ("ctx_0", "ctx_1", "tp"))
    return jax.shard_map(
        on_device,
        mesh=finer,
        in_specs=(
            P(None, CTX),
            P(None, CTX),
            P(None, CTX, "tp"),
            P(None, CTX, "tp"),
            P(None, CTX, "tp"),
            P(None, "tp", CTX),
            P(None, None, "tp", CTX, None),
            P(None, None, "tp", CTX, None),
            P(),
        ),
        out_specs=P(None, CTX),
        check_vma=False,
    )
```

profile of v0, /device:TPU:1, one launch (start us, length us, event | category | flops | bytes accessed | tf_op | source)
XLA Modules:
  0.0 402.6 jit_solution(12077693957421392516)
XLA Ops:
  5.5 1.5 fusion.22
  7.0 14.6 %all-reduce.15 = (f32[8,1024]{1,0:T(8,128)S(1)}, f32[8]{0:T(128)S(1)}) all-reduce(f32[8,1024]{1,0:T(8,128)S(1)} %fusion.22, f32[8]{0:T(128)S(1)} %fusion.65), channel_id=1, replica_groups=mesh['ctx_0'=4,'ctx_1'=4,'tp'=8] {'ctx_0'}, use_global_device_ids=true, to_apply=%region_0.0 | all-reduce | flops 8200 | bytes 65600 | tf_op jit(solution)/shard_map/psum | solution.py:20
  21.7 14.0 %all-reduce.7 = (f32[8,1024]{1,0:T(8,128)S(1)}, f32[8]{0:T(128)S(1)}) all-reduce(f32[8,1024]{1,0:T(8,128)S(1)} %get-tuple-element.51, f32[8]{0:T(128)S(1)} %get-tuple-element.52), channel_id=1, replica_groups=mesh['ctx_0'=4,'ctx_1'=4,'tp'=8] {'ctx_1'}, use_global_device_ids=true, to_apply=%region_1.0 | all-reduce | flops 8200 | bytes 65600 | tf_op jit(solution)/shard_map/psum | solution.py:20
  37.1 6.0 %pmax.56 = f32[8,1,8]{2,0,1:T(8,128)S(1)} all-reduce(f32[8,1,8]{2,0,1:T(8,128)S(1)} %bitcast.314), channel_id=1, replica_groups=mesh['ctx_0'=4,'ctx_1'=4,'tp'=8] {'ctx_0'}, use_global_device_ids=true, to_apply=%region_6.0 | all-reduce | flops 64 | bytes 512 | tf_op jit(solution)/shard_map/pmax | solution.py:25
  43.2 6.0 %pmax.57 = f32[8,1,8]{2,0,1:T(8,128)S(1)} all-reduce(f32[8,1,8]{2,0,1:T(8,128)S(1)} %pmax.56), channel_id=1, replica_groups=mesh['ctx_0'=4,'ctx_1'=4,'tp'=8] {'ctx_1'}, use_global_device_ids=true, to_apply=%region_7.0 | all-reduce | flops 64 | bytes 512 | tf_op jit(solution)/shard_map/pmax | solution.py:25
  50.5 12.8 %all-reduce.14 = (f32[8,1,8]{2,0,1:T(8,128)S(1)}, f32[8,128]{1,0:T(8,128)S(1)}, f32[8,128]{1,0:T(8,128)S(1)}, f32[8,1,8,128]{3,2,0,1:T(8,128)S(1)}) all-reduce(f32[8,1,8]{2,0,1:T(8,128)S(1)} %get-tuple-element.88, f32[8,128]{1,0:T(8,128)S(1)} %fusion.46, ...), channel_id=1, replica_groups=mesh['ctx_0'=4,'ctx_1'=4,'tp'=8] {'ctx_0'}, use_global_device_ids=true, to_apply=%region_15.16 | all-reduce | flops 10304 | bytes 82432 | tf_op jit(solution)/shard_map/psum | solution.py:20
  63.3 13.0 %all-reduce.6 = (f32[8,1,8]{2,0,1:T(8,128)S(1)}, f32[8,128]{1,0:T(8,128)S(1)}, f32[8,128]{1,0:T(8,128)S(1)}, f32[8,1,8,128]{3,2,0,1:T(8,128)S(1)}) all-reduce(f32[8,1,8]{2,0,1:T(8,128)S(1)} %get-tuple-element.47, f32[8,128]{1,0:T(8,128)S(1)} %get-tuple-element.48, ...), channel_id=1, replica_groups=mesh['ctx_0'=4,'ctx_1'=4,'tp'=8] {'ctx_1'}, use_global_device_ids=true, to_apply=%region_16.17 | all-reduce | flops 10304 | bytes 82432 | tf_op jit(solution)/shard_map/psum | solution.py:20
  78.4 32.6 %all-gather = f32[64,512]{1,0:T(8,128)S(1)} all-gather(f32[8,512]{1,0:T(8,128)S(1)} %fusion.20), channel_id=2, replica_groups=mesh['ctx_0'=4,'ctx_1'=4,'tp'=8] {'tp'}, dimensions={0}, use_global_device_ids=true | all-gather | bytes 147456 | tf_op jit(solution)/shard_map/all_gather | solution.py:30
  111.4 1.5 fusion.18
  112.9 11.5 %all-reduce.13 = (f32[8,1024]{1,0:T(8,128)S(1)}, f32[8]{0:T(128)S(1)}) all-reduce(f32[8,1024]{1,0:T(8,128)S(1)} %fusion.18, f32[8]{0:T(128)S(1)} %get-tuple-element.67), channel_id=1, replica_groups=mesh['ctx_0'=4,'ctx_1'=4,'tp'=8] {'ctx_0'}, use_global_device_ids=true, to_apply=%region_18.19 | all-reduce | flops 8200 | bytes 65600 | tf_op jit(solution)/shard_map/psum | solution.py:20
  124.4 11.2 %all-reduce.5 = (f32[8,1024]{1,0:T(8,128)S(1)}, f32[8]{0:T(128)S(1)}) all-reduce(f32[8,1024]{1,0:T(8,128)S(1)} %get-tuple-element.45, f32[8]{0:T(128)S(1)} %get-tuple-element.46), channel_id=1, replica_groups=mesh['ctx_0'=4,'ctx_1'=4,'tp'=8] {'ctx_1'}, use_global_device_ids=true, to_apply=%region_19.20 | all-reduce | flops 8200 | bytes 65600 | tf_op jit(solution)/shard_map/psum | solution.py:20
  136.1 7.6 %pmax.58 = f32[8,1,8]{2,0,1:T(8,128)S(1)} all-reduce(f32[8,1,8]{2,0,1:T(8,128)S(1)} %bitcast.315), channel_id=1, replica_groups=mesh['ctx_0'=4,'ctx_1'=4,'tp'=8] {'ctx_0'}, use_global_device_ids=true, to_apply=%region_24.25 | all-reduce | flops 64 | bytes 512 | tf_op jit(solution)/shard_map/pmax | solution.py:25
  143.7 7.6 %pmax.59 = f32[8,1,8]{2,0,1:T(8,128)S(1)} all-reduce(f32[8,1,8]{2,0,1:T(8,128)S(1)} %pmax.58), channel_id=1, replica_groups=mesh['ctx_0'=4,'ctx_1'=4,'tp'=8] {'ctx_1'}, use_global_device_ids=true, to_apply=%region_25.26 | all-reduce | flops 64 | bytes 512 | tf_op jit(solution)/shard_map/pmax | solution.py:25
  151.7 11.5 %all-reduce.12 = (f32[8,1,8]{2,0,1:T(8,128)S(1)}, f32[8,128]{1,0:T(8,128)S(1)}, f32[8,128]{1,0:T(8,128)S(1)}, f32[8,1,8,128]{3,2,0,1:T(8,128)S(1)}) all-reduce(f32[8,1,8]{2,0,1:T(8,128)S(1)} %get-tuple-element.83, f32[8,128]{1,0:T(8,128)S(1)} %fusion.42, ...), channel_id=1, replica_groups=mesh['ctx_0'=4,'ctx_1'=4,'tp'=8] {'ctx_0'}, use_global_device_ids=true, to_apply=%region_33.34 | all-reduce | flops 10304 | bytes 82432 | tf_op jit(solution)/shard_map/psum | solution.py:20
  163.3 11.7 %all-reduce.4 = (f32[8,1,8]{2,0,1:T(8,128)S(1)}, f32[8,128]{1,0:T(8,128)S(1)}, f32[8,128]{1,0:T(8,128)S(1)}, f32[8,1,8,128]{3,2,0,1:T(8,128)S(1)}) all-reduce(f32[8,1,8]{2,0,1:T(8,128)S(1)} %get-tuple-element.41, f32[8,128]{1,0:T(8,128)S(1)} %get-tuple-element.42, ...), channel_id=1, replica_groups=mesh['ctx_0'=4,'ctx_1'=4,'tp'=8] {'ctx_1'}, use_global_device_ids=true, to_apply=%region_34.35 | all-reduce | flops 10304 | bytes 82432 | tf_op jit(solution)/shard_map/psum | solution.py:20
  177.0 29.8 %all-gather.1 = f32[64,512]{1,0:T(8,128)S(1)} all-gather(f32[8,512]{1,0:T(8,128)S(1)} %fusion.16), channel_id=3, replica_groups=mesh['ctx_0'=4,'ctx_1'=4,'tp'=8] {'tp'}, dimensions={0}, use_global_device_ids=true | all-gather | bytes 147456 | tf_op jit(solution)/shard_map/all_gather | solution.py:30
  207.2 1.5 fusion.14
  208.7 12.7 %all-reduce.11 = (f32[8,1024]{1,0:T(8,128)S(1)}, f32[8]{0:T(128)S(1)}) all-reduce(f32[8,1024]{1,0:T(8,128)S(1)} %fusion.14, f32[8]{0:T(128)S(1)} %get-tuple-element.55), channel_id=1, replica_groups=mesh['ctx_0'=4,'ctx_1'=4,'tp'=8] {'ctx_0'}, use_global_device_ids=true, to_apply=%region_36.37 | all-reduce | flops 8200 | bytes 65600 | tf_op jit(solution)/shard_map/psum | solution.py:20
  221.4 12.6 %all-reduce.3 = (f32[8,1024]{1,0:T(8,128)S(1)}, f32[8]{0:T(128)S(1)}) all-reduce(f32[8,1024]{1,0:T(8,128)S(1)} %get-tuple-element.39, f32[8]{0:T(128)S(1)} %get-tuple-element.40), channel_id=1, replica_groups=mesh['ctx_0'=4,'ctx_1'=4,'tp'=8] {'ctx_1'}, use_global_device_ids=true, to_apply=%region_37.38 | all-reduce | flops 8200 | bytes 65600 | tf_op jit(solution)/shard_map/psum | solution.py:20
  234.6 6.1 %pmax.60 = f32[8,1,8]{2,0,1:T(8,128)S(1)} all-reduce(f32[8,1,8]{2,0,1:T(8,128)S(1)} %bitcast.316), channel_id=1, replica_groups=mesh['ctx_0'=4,'ctx_1'=4,'tp'=8] {'ctx_0'}, use_global_device_ids=true, to_apply=%region_42.43 | all-reduce | flops 64 | bytes 512 | tf_op jit(solution)/shard_map/pmax | solution.py:25
  240.7 6.2 %pmax.61 = f32[8,1,8]{2,0,1:T(8,128)S(1)} all-reduce(f32[8,1,8]{2,0,1:T(8,128)S(1)} %pmax.60), channel_id=1, replica_groups=mesh['ctx_0'=4,'ctx_1'=4,'tp'=8] {'ctx_1'}, use_global_device_ids=true, to_apply=%region_43.44 | all-reduce | flops 64 | bytes 512 | tf_op jit(solution)/shard_map/pmax | solution.py:25
  247.3 12.4 %all-reduce.10 = (f32[8,1,8]{2,0,1:T(8,128)S(1)}, f32[8,128]{1,0:T(8,128)S(1)}, f32[8,128]{1,0:T(8,128)S(1)}, f32[8,1,8,128]{3,2,0,1:T(8,128)S(1)}) all-reduce(f32[8,1,8]{2,0,1:T(8,128)S(1)} %get-tuple-element.78, f32[8,128]{1,0:T(8,128)S(1)} %fusion.38, ...), channel_id=1, replica_groups=mesh['ctx_0'=4,'ctx_1'=4,'tp'=8] {'ctx_0'}, use_global_device_ids=true, to_apply=%region_51.52 | all-reduce | flops 10304 | bytes 82432 | tf_op jit(solution)/shard_map/psum | solution.py:20
  259.7 13.2 %all-reduce.2 = (f32[8,1,8]{2,0,1:T(8,128)S(1)}, f32[8,128]{1,0:T(8,128)S(1)}, f32[8,128]{1,0:T(8,128)S(1)}, f32[8,1,8,128]{3,2,0,1:T(8,128)S(1)}) all-reduce(f32[8,1,8]{2,0,1:T(8,128)S(1)} %get-tuple-element.35, f32[8,128]{1,0:T(8,128)S(1)} %get-tuple-element.36, ...), channel_id=1, replica_groups=mesh['ctx_0'=4,'ctx_1'=4,'tp'=8] {'ctx_1'}, use_global_device_ids=true, to_apply=%region_52.53 | all-reduce | flops 10304 | bytes 82432 | tf_op jit(solution)/shard_map/psum | solution.py:20
  274.9 31.2 %all-gather.2 = f32[64,512]{1,0:T(8,128)S(1)} all-gather(f32[8,512]{1,0:T(8,128)S(1)} %fusion.12), channel_id=4, replica_groups=mesh['ctx_0'=4,'ctx_1'=4,'tp'=8] {'tp'}, dimensions={0}, use_global_device_ids=true | all-gather | bytes 147456 | tf_op jit(solution)/shard_map/all_gather | solution.py:30
  306.5 1.5 fusion.10
  308.0 11.5 %all-reduce.9 = (f32[8,1024]{1,0:T(8,128)S(1)}, f32[8]{0:T(128)S(1)}) all-reduce(f32[8,1024]{1,0:T(8,128)S(1)} %fusion.10, f32[8]{0:T(128)S(1)} %get-tuple-element.53), channel_id=1, replica_groups=mesh['ctx_0'=4,'ctx_1'=4,'tp'=8] {'ctx_0'}, use_global_device_ids=true, to_apply=%region_54.55 | all-reduce | flops 8200 | bytes 65600 | tf_op jit(solution)/shard_map/psum | solution.py:20
  319.5 11.2 %all-reduce.1 = (f32[8,1024]{1,0:T(8,128)S(1)}, f32[8]{0:T(128)S(1)}) all-reduce(f32[8,1024]{1,0:T(8,128)S(1)} %get-tuple-element.33, f32[8]{0:T(128)S(1)} %get-tuple-element.34), channel_id=1, replica_groups=mesh['ctx_0'=4,'ctx_1'=4,'tp'=8] {'ctx_1'}, use_global_device_ids=true, to_apply=%region_55.56 | all-reduce | flops 8200 | bytes 65600 | tf_op jit(solution)/shard_map/psum | solution.py:20
  331.2 7.7 %pmax.62 = f32[8,1,8]{2,0,1:T(8,128)S(1)} all-reduce(f32[8,1,8]{2,0,1:T(8,128)S(1)} %bitcast.313), channel_id=1, replica_groups=mesh['ctx_0'=4,'ctx_1'=4,'tp'=8] {'ctx_0'}, use_global_device_ids=true, to_apply=%region_60.61 | all-reduce | flops 64 | bytes 512 | tf_op jit(solution)/shard_map/pmax | solution.py:25
  338.9 7.3 %pmax.63 = f32[8,1,8]{2,0,1:T(8,128)S(1)} all-reduce(f32[8,1,8]{2,0,1:T(8,128)S(1)} %pmax.62), channel_id=1, replica_groups=mesh['ctx_0'=4,'ctx_1'=4,'tp'=8] {'ctx_1'}, use_global_device_ids=true, to_apply=%region_61.62 | all-reduce | flops 64 | bytes 512 | tf_op jit(solution)/shard_map/pmax | solution.py:25
  346.6 11.9 %all-reduce.8 = (f32[8,1,8]{2,0,1:T(8,128)S(1)}, f32[8,128]{1,0:T(8,128)S(1)}, f32[8,128]{1,0:T(8,128)S(1)}, f32[8,1,8,128]{3,2,0,1:T(8,128)S(1)}) all-reduce(f32[8,1,8]{2,0,1:T(8,128)S(1)} %get-tuple-element.73, f32[8,128]{1,0:T(8,128)S(1)} %fusion.34, ...), channel_id=1, replica_groups=mesh['ctx_0'=4,'ctx_1'=4,'tp'=8] {'ctx_0'}, use_global_device_ids=true, to_apply=%region_69.70 | all-reduce | flops 10304 | bytes 82432 | tf_op jit(solution)/shard_map/psum | solution.py:20
  358.4 11.2 %all-reduce = (f32[8,1,8]{2,0,1:T(8,128)S(1)}, f32[8,128]{1,0:T(8,128)S(1)}, f32[8,128]{1,0:T(8,128)S(1)}, f32[8,1,8,128]{3,2,0,1:T(8,128)S(1)}) all-reduce(f32[8,1,8]{2,0,1:T(8,128)S(1)} %get-tuple-element.29, f32[8,128]{1,0:T(8,128)S(1)} %get-tuple-element.30, ...), channel_id=1, replica_groups=mesh['ctx_0'=4,'ctx_1'=4,'tp'=8] {'ctx_1'}, use_global_device_ids=true, to_apply=%region_70.71 | all-reduce | flops 10304 | bytes 82432 | tf_op jit(solution)/shard_map/psum | solution.py:20
  371.7 30.3 %all-gather.3 = f32[64,512]{1,0:T(8,128)S(1)} all-gather(f32[8,512]{1,0:T(8,128)S(1)} %fusion.8), channel_id=5, replica_groups=mesh['ctx_0'=4,'ctx_1'=4,'tp'=8] {'tp'}, dimensions={0}, use_global_device_ids=true | all-gather | bytes 147456 | tf_op jit(solution)/shard_map/all_gather | solution.py:30
  (99 shorter events, 21.1 us)
Async XLA Ops:
  0.0 111.0 %copy-start.4 = (bf16[8,512]{1,0:T(8,128)(2,1)S(1)}, bf16[8,512]{1,0:T(8,128)(2,1)}, u32[]{:S(2)}) copy-start(bf16[8,512]{1,0:T(8,128)(2,1)} %param.9) | copy-start | bytes 24580
  0.0 111.2 %copy-start.2 = (bf16[4,512,128]{2,1,0:T(8,128)(2,1)S(1)}, bf16[4,512,128]{2,1,0:T(8,128)(2,1)}, u32[]{:S(2)}) copy-start(bf16[4,512,128]{2,1,0:T(8,128)(2,1)} %param.13) | copy-start | bytes 1572868
  0.0 111.3 %copy-start.3 = (bf16[4,512,128]{2,1,0:T(8,128)(2,1)S(1)}, bf16[4,512,128]{2,1,0:T(8,128)(2,1)}, u32[]{:S(2)}) copy-start(bf16[4,512,128]{2,1,0:T(8,128)(2,1)} %param.12) | copy-start | bytes 1572868
  0.0 151.5 %copy-start.1 = (bf16[4,8,1,128,128]{4,3,2,1,0:T(8,128)(2,1)S(1)}, bf16[4,8,1,128,128]{4,3,2,1,0:T(8,128)(2,1)}, u32[]{:S(2)}) copy-start(bf16[4,8,1,128,128]{4,3,2,1,0:T(8,128)(2,1)} %param.16) | copy-start | bytes 3145732
  0.0 135.8 %copy-start = (bf16[4,8,1,128,128]{4,3,2,1,0:T(8,128)(2,1)S(1)}, bf16[4,8,1,128,128]{4,3,2,1,0:T(8,128)(2,1)}, u32[]{:S(2)}) copy-start(bf16[4,8,1,128,128]{4,3,2,1,0:T(8,128)(2,1)} %param.15) | copy-start | bytes 3145732
where the time goes:
time: 404 us; the launch traced here: 403 us
  blocking collectives  375 us (93%)
  matrix products  19.7 us (5%)
  other arithmetic  7.17 us (2%)
    psum x16, blocking collectives, over_axes(): return functools.reduce(lax.psum, axes, shard)  197 us
    all_gather x4, blocking collectives, over_pieces(): return lax.all_gather(shard, axis).sum(0)  124 us
    pmax x8, blocking collectives, one_axis_at_a_time(): shard = lax.pmax(shard, axis)  54.4 us

commit v1 on v0

v1 whole, which is shorter than its diff:
```python
import functools
import math

import jax
import jax.numpy as jnp
import numpy as np
from jax import lax
from jax.experimental import pallas as pl
from jax.experimental.pallas import tpu as pltpu
from jax.sharding import PartitionSpec as P

MESH = pl.DeviceIdType.MESH
LAYERS = 4
B = 8
HD = 128
HALF = 64
D = 8192
SEG = 128
FILL = -1e30
EPS = 1e-5
ROPE_BASE = 500000.0
F32 = jnp.float32
BF16 = jnp.bfloat16
QA = 5 * HD
QB = 5 * HD
PART = 6 * HD


def tile(value, i):
    return value[:, i * HD : (i + 1) * HD]


def kernel(
    hidden, gains, w_query, w_key, w_value, w_out, key_cache, value_cache, lengths, freq,
    out,
    hbuf, gbuf, wqkv, wo, kbuf, vbuf, fbuf, snd, rcv, tpb,
    lsem, psem, fsem, ssem, rsem, tssem, trsem,
):
    c = lax.axis_index("ctx")
    t = lax.axis_index("tp")
    y, x = c // 4, lax.rem(c, 4)

    def weight_loads(l):
        return (
            pltpu.make_async_copy(w_query.at[l], wqkv.at[l, :, pl.ds(0, 8 * HD)], lsem.at[l, 0]),
            pltpu.make_async_copy(w_key.at[l], wqkv.at[l, :, pl.ds(8 * HD, HD)], lsem.at[l, 1]),
            pltpu.make_async_copy(w_value.at[l], wqkv.at[l, :, pl.ds(9 * HD, HD)], lsem.at[l, 2]),
            pltpu.make_async_copy(key_cache.at[l, :, 0], kbuf.at[l], lsem.at[l, 3]),
            pltpu.make_async_copy(value_cache.at[l, :, 0], vbuf.at[l], lsem.at[l, 4]),
            pltpu.make_async_copy(w_out.at[l], wo.at[l], lsem.at[l, 5]),
        )

    small = (
        pltpu.make_async_copy(hidden, hbuf, psem.at[0]),
        pltpu.make_async_copy(gains, gbuf, psem.at[1]),
        pltpu.make_async_copy(freq, fbuf, psem.at[2]),
    )
    for copy in small:
        copy.start()
    loads = [weight_loads(l) for l in range(LAYERS)]
    for group in loads:
        for copy in group:
            copy.start()

    along_x = [(y * 4 + lax.rem(x + d, 4), t) for d in (1, 2, 3)]
    along_y = [(lax.rem(y + d, 4) * 4 + x, t) for d in (1, 2, 3)]
    along_t = [(c, lax.rem(t + d, 8)) for d in range(1, 8)]
    barrier = pltpu.get_barrier_semaphore()
    for peer in along_x + along_y + along_t:
        pl.semaphore_signal(barrier, inc=1, device_id=peer, device_id_type=MESH)

    lane = lax.broadcasted_iota(jnp.int32, (B, HD), 1)
    row = lax.broadcasted_iota(jnp.int32, (B, HD), 0)
    length = jnp.zeros((B, HD), jnp.int32)
    for b in range(B):
        length = jnp.where(row == b, lengths[b], length)
    usable = c * SEG + lane < length
    small[2].wait()
    angle = length.astype(F32) * fbuf[...]
    cosine = jnp.cos(angle)
    sine = jnp.where(lane < HALF, -jnp.sin(angle), jnp.sin(angle))
    small[0].wait()
    small[1].wait()
    stream = hbuf[...].astype(F32)
    pl.semaphore_wait(barrier, 13)

    def exchange(l, phase, width, peers):
        copies = []
        for i in (1, 0, 2):
            copy = pltpu.make_async_remote_copy(
                src_ref=snd.at[l, phase, :, pl.ds(0, width)],
                dst_ref=rcv.at[l, phase, i, :, pl.ds(0, width)],
                send_sem=ssem.at[l, phase, i],
                recv_sem=rsem.at[l, phase, i],
                device_id=peers[i],
                device_id_type=MESH,
            )
            copy.start()
            copies.append(copy)
        return copies

    def arrive(copies):
        for copy in copies:
            copy.wait_recv()

    def total(l, phase, width):
        own = snd[l, phase, :, :width]
        got = [rcv[l, phase, i, :, :width] for i in range(3)]
        return (own + got[0]) + (got[1] + got[2])

    def merge(l, phase, fresh=None):
        outs = [snd[l, phase, :, : 4 * HD]] + [rcv[l, phase, i, :, : 4 * HD] for i in range(3)]
        stats = [snd[l, phase, :, 4 * HD : 5 * HD]] + [
            rcv[l, phase, i, :, 4 * HD : 5 * HD] for i in range(3)
        ]
        sums = [pltpu.roll(s, HALF, 1) for s in stats]
        top = jnp.maximum(jnp.maximum(stats[0], stats[1]), jnp.maximum(stats[2], stats[3]))
        if fresh is not None:
            top = jnp.maximum(top, fresh[0])
        scale = [jnp.exp(s - top) for s in stats]
        whole = (scale[0] * sums[0] + scale[1] * sums[1]) + (scale[2] * sums[2] + scale[3] * sums[3])
        if fresh is not None:
            new = jnp.exp(fresh[0] - top)
            whole = whole + new
            scale = [s / whole for s in scale]
            new = new.astype(BF16).astype(F32) / whole
        result = []
        for j in range(4):
            parts = [jnp.broadcast_to(s[:, j : j + 1], (B, HD)) * tile(o, j) for s, o in zip(scale, outs)]
            joined = (parts[0] + parts[1]) + (parts[2] + parts[3])
            if fresh is not None:
                joined = joined + jnp.broadcast_to(new[:, j : j + 1], (B, HD)) * fresh[1]
            result.append(joined)
        return result, top, whole

    sent = []
    for l in range(LAYERS):
        load = loads[l]
        gain = gbuf[l : l + 1, :].astype(F32)
        scaled = (stream * gain).astype(BF16)
        squares = stream * stream
        squares = (tile(squares, 0) + tile(squares, 1)) + (tile(squares, 2) + tile(squares, 3))
        for i in range(3):
            load[i].wait()
        snd[l, 0, :, :QA] = jnp.dot(scaled, wqkv[l, :, :QA], preferred_element_type=F32)
        snd[l, 0, :, QA : QA + HD] = squares
        a1 = exchange(l, 0, QA + HD, along_x)
        snd[l, 1, :, :QB] = jnp.dot(scaled, wqkv[l, :, QA:], preferred_element_type=F32)
        b1 = exchange(l, 1, QB, along_y)
        arrive(a1)
        snd[l, 2, :, : QA + HD] = total(l, 0, QA + HD)
        a2 = exchange(l, 2, QA + HD, along_y)
        arrive(b1)
        snd[l, 3, :, :QB] = total(l, 1, QB)
        b2 = exchange(l, 3, QB, along_x)
        load[3].wait()
        load[4].wait()
        arrive(a2)
        first = total(l, 2, QA + HD)
        inverse = lax.rsqrt(jnp.sum(tile(first, 5), axis=1, keepdims=True) / D + EPS)
        cos_l, sin_l = cosine * inverse, sine * inverse

        def rotate(u):
            return u * cos_l + pltpu.roll(u, HALF, 1) * sin_l

        arrive(b2)
        second = total(l, 3, QB)
        raw = [tile(first, i) for i in range(5)] + [tile(second, i) for i in range(3)]
        query = jnp.concatenate([rotate(u) for u in raw], axis=0).astype(BF16)
        new_key = rotate(tile(second, 3)).astype(BF16).astype(F32)
        new_value = (tile(second, 4) * inverse).astype(BF16).astype(F32)

        keys = kbuf[l].reshape(B * SEG, HD)
        score = lax.dot_general(query, keys, (((1,), (1,)), ((), ())), preferred_element_type=F32)
        probs, tops, sums = [], [], []
        for h in range(8):
            block = score[h * B : (h + 1) * B]
            s = tile(block, 0)
            for b in range(1, B):
                s = jnp.where(row == b, tile(block, b), s)
            s = jnp.where(usable, s * (1.0 / math.sqrt(HD)), FILL)
            top = jnp.max(s, axis=1, keepdims=True)
            p = jnp.where(usable, jnp.exp(s - top), 0.0)
            tops.append(top)
            sums.append(jnp.sum(p, axis=1, keepdims=True))
            probs.append(jnp.concatenate([jnp.where(row == b, p, 0.0) for b in range(B)], axis=1))
        probs = jnp.concatenate(probs, axis=0).astype(BF16)
        mixed = jnp.dot(probs, vbuf[l].reshape(B * SEG, HD), preferred_element_type=F32)

        def store_half(phase, start):
            stats = jnp.zeros((B, HD), F32)
            for j in range(4):
                h = start + j
                snd[l, phase, :, j * HD : (j + 1) * HD] = mixed[h * B : (h + 1) * B]
                stats = jnp.where(lane == j, tops[h], stats)
                stats = jnp.where(lane == HALF + j, sums[h], stats)
            snd[l, phase, :, 4 * HD : 5 * HD] = stats

        store_half(4, 0)
        a3 = exchange(l, 4, 5 * HD, along_x)
        store_half(5, 4)
        b3 = exchange(l, 5, 5 * HD, along_y)
        own = [jnp.zeros((B, HD), F32), jnp.zeros((B, HD), F32)]
        for h in range(8):
            dot = jnp.sum(query[h * B : (h + 1) * B].astype(F32) * new_key, axis=1, keepdims=True)
            own[h // 4] = jnp.where(lane == h % 4, dot * (1.0 / math.sqrt(HD)), own[h // 4])

        def pass_on(phase_in, phase_out):
            joined, top, whole = merge(l, phase_in)
            for j in range(4):
                snd[l, phase_out, :, j * HD : (j + 1) * HD] = joined[j]
            snd[l, phase_out, :, 4 * HD : 5 * HD] = jnp.where(lane < HALF, top, pltpu.roll(whole, HALF, 1))

        arrive(a3)
        pass_on(4, 6)
        a4 = exchange(l, 6, 5 * HD, along_y)
        arrive(b3)
        pass_on(5, 7)
        b4 = exchange(l, 7, 5 * HD, along_x)
        load[5].wait()
        arrive(a4)
        context = jnp.concatenate(merge(l, 6, (own[0], new_value))[0], axis=1).astype(BF16)
        head_part = jnp.dot(context, wo[l, : 4 * HD, :], preferred_element_type=F32)
        arrive(b4)
        context = jnp.concatenate(merge(l, 7, (own[1], new_value))[0], axis=1).astype(BF16)
        head_part = head_part + jnp.dot(context, wo[l, 4 * HD :, :], preferred_element_type=F32)

        tpb[l, t] = head_part
        copies = []
        for d in (4, 5, 3, 2, 6, 1, 7):
            copy = pltpu.make_async_remote_copy(
                src_ref=tpb.at[l, t],
                dst_ref=tpb.at[l, t],
                send_sem=tssem.at[l, d - 1],
                recv_sem=trsem.at[l, d - 1],
                device_id=along_t[d - 1],
                device_id_type=MESH,
            )
            copy.start()
            copies.append(copy)
        sent += a1 + b1 + a2 + b2 + a3 + b3 + a4 + b4 + copies
        arrive(copies)
        gathered = [tpb[l, i] for i in range(8)]
        while len(gathered) > 1:
            gathered = [gathered[i] + gathered[i + 1] for i in range(0, len(gathered), 2)]
        stream = stream + gathered[0]
    out[...] = stream
    for copy in sent:
        copy.wait_send()


def on_device(hidden, norm_gains, w_query, w_key, w_value, w_out, key_cache, value_cache, lengths):
    exponents = np.arange(HALF, dtype=np.float32) * np.float32(2.0 / HD)
    freq = np.exp(-exponents.astype(np.float64) * math.log(ROPE_BASE)).astype(np.float32)
    freq = jnp.asarray(np.tile(np.concatenate([freq, freq])[None, :], (B, 1)))
    hbm = pl.BlockSpec(memory_space=pl.ANY)
    return pl.pallas_call(
        kernel,
        out_shape=jax.ShapeDtypeStruct((B, 512), F32),
        in_specs=[hbm] * 8 + [pl.BlockSpec(memory_space=pltpu.SMEM), hbm],
        out_specs=pl.BlockSpec(memory_space=pltpu.VMEM),
        scratch_shapes=[
            pltpu.VMEM((B, 512), BF16),
            pltpu.VMEM((LAYERS, 512), BF16),
            pltpu.VMEM((LAYERS, 512, 10 * HD), BF16),
            pltpu.VMEM((LAYERS, 8 * HD, 512), BF16),
            pltpu.VMEM((LAYERS, B, SEG, HD), BF16),
            pltpu.VMEM((LAYERS, B, SEG, HD), BF16),
            pltpu.VMEM((B, HD), F32),
            pltpu.VMEM((LAYERS, 8, B, PART), F32),
            pltpu.VMEM((LAYERS, 8, 3, B, PART), F32),
            pltpu.VMEM((LAYERS, 8, B, 512), F32),
            pltpu.SemaphoreType.DMA((LAYERS, 6)),
            pltpu.SemaphoreType.DMA((3,)),
            pltpu.SemaphoreType.DMA((1,)),
            pltpu.SemaphoreType.DMA((LAYERS, 8, 3)),
            pltpu.SemaphoreType.DMA((LAYERS, 8, 3)),
            pltpu.SemaphoreType.DMA((LAYERS, 7)),
            pltpu.SemaphoreType.DMA((LAYERS, 7)),
        ],
        compiler_params=pltpu.CompilerParams(
            collective_id=0, has_side_effects=True, vmem_limit_bytes=60 * 1024 * 1024
        ),
    )(hidden, norm_gains, w_query, w_key, w_value, w_out, key_cache, value_cache, lengths, freq)


def solution(mesh):
    return jax.shard_map(
        on_device,
        mesh=mesh,
        in_specs=(
            P(None, "ctx"),
            P(None, "ctx"),
            P(None, "ctx", "tp"),
            P(None, "ctx", "tp"),
            P(None, "ctx", "tp"),
            P(None, "tp", "ctx"),
            P(None, None, "tp", "ctx", None),
            P(None, None, "tp", "ctx", None),
            P(),
        ),
        out_specs=P(None, "ctx"),
        check_vma=False,
    )
```

time: 404 us -> 94.2 us (0.23)
  blocking collectives: 375 us -> 0 us
  Pallas kernels: 0 us -> 92.7 us
  matrix products: 19.7 us -> 0 us
  other arithmetic: 7.17 us -> 0 us
    psum x16 -> x0, blocking collectives: 197 us -> none  [over_axes(): return functools.reduce(lax.psum, axes, shard)]
    all_gather x4 -> x0, blocking collectives: 124 us -> none  [over_pieces(): return lax.all_gather(shard, axis).sum(0)]
    pallas_call x0 -> x1, Pallas kernels: none -> 92.7 us  [on_device(): pl.pallas_call(kernel, out_shape=jax.ShapeDtypeStruct((B, 512), F32), in_...]
    pmax x8 -> x0, blocking collectives: 54.4 us -> none  [one_axis_at_a_time(): shard = lax.pmax(shard, axis)]
    dot_general x28 -> x0, matrix products: 19.7 us -> none  [the longest x4 5.92 us: on_device(): jnp.dot(scaled, w_query[layer_idx], preferred_element_type=jnp.float32)]
where the time goes in v1:
time: 94.2 us; the launch traced here: 94 us
  Pallas kernels  92.7 us (98%)
  local copies, waits for them, and re-layouts  1.32 us (1%)
    pallas_call x1, Pallas kernels, on_device(): pl.pallas_call(kernel, out_shape=jax.ShapeDtypeStruct((B, 512), F32), in_...  92.7 us

profile of v1, /device:TPU:1, one launch (start us, length us, event | category | flops | bytes accessed | tf_op | source)
XLA Modules:
  0.0 94.0 jit_solution(15175804518693011768)
XLA Ops:
  0.0 92.7 %shard_map.100 = f32[8,512]{1,0:T(8,128)} custom-call(bf16[8,512]{1,0:T(8,128)(2,1)} %hidden.1, bf16[4,512]{1,0:T(4,128)(2,1)} %gains.1, bf16[4,512,1024]{2,1,0:T(8,128)(2,1)} %w_query.1, bf16[4,512,128]{2,1,0:T(8,128)(2,1)} %w_key.1, bf16[4,512,128]{2,1,0:T(8,128)(2,1)} %w_value.1, bf16[4,1024,512]{2,1,0:T(8,128)(2,1)} %w_out.1, ...), custom_call_target="tpu_custom_call" | custom-call | tf_op jit(solution)/shard_map/pallas_call | solution.py:257
  92.7 1.3 %copy.12 = f32[8,512]{1,0:T(8,128)} copy(f32[8,512]{1,0:T(8,128)} %shard_map.100) | data formatting | bytes 32768

commit v2 on v1

--- a/solution.py
+++ b/solution.py
@@ -24,21 +24,32 @@
 QA = 5 * HD
 QB = 5 * HD
 PART = 6 * HD
+PLANE_ORDER = (10, 6, 9, 11, 14, 2, 8, 5, 7, 13, 15, 1, 3, 4, 12)
+UNIT = 32
+PLAN = (2, 1, 2, 1, 3, 3, 2, 2, 2, 2, 2, 2, 0, 0)
 
 
 def tile(value, i):
     return value[:, i * HD : (i + 1) * HD]
+
+
+def add_up(terms):
+    while len(terms) > 1:
+        pairs = [terms[i] + terms[i + 1] for i in range(0, len(terms) - 1, 2)]
+        terms = pairs + terms[len(terms) - len(terms) % 2 :]
+    return terms[0]
 
 
 def kernel(
     hidden, gains, w_query, w_key, w_value, w_out, key_cache, value_cache, lengths, freq,
     out,
-    hbuf, gbuf, wqkv, wo, kbuf, vbuf, fbuf, snd, rcv, tpb,
-    lsem, psem, fsem, ssem, rsem, tssem, trsem,
+    hbuf, gbuf, wqkv, wo, kbuf, vbuf, fbuf, snd, rcv, tpb, keys_t, stage, moved, values, qsnd, qrcv, orcv,
+    lsem, psem, ssem, rsem, tssem, trsem, bssem, brsem, qssem, qrsem, ossem, orsem,
 ):
     c = lax.axis_index("ctx")
     t = lax.axis_index("tp")
     y, x = c // 4, lax.rem(c, 4)
+    mine, part = lax.rem(c, 8), c // 8
 
     def weight_loads(l):
         return (
@@ -65,8 +76,9 @@
     along_x = [(y * 4 + lax.rem(x + d, 4), t) for d in (1, 2, 3)]
     along_y = [(lax.rem(y + d, 4) * 4 + x, t) for d in (1, 2, 3)]
     along_t = [(c, lax.rem(t + d, 8)) for d in range(1, 8)]
+    plane = [(lax.rem(y + d // 4, 4) * 4 + lax.rem(x + d % 4, 4), t) for d in range(1, 16)]
     barrier = pltpu.get_barrier_semaphore()
-    for peer in along_x + along_y + along_t:
+    for peer in plane + along_t:
         pl.semaphore_signal(barrier, inc=1, device_id=peer, device_id_type=MESH)
 
     lane = lax.broadcasted_iota(jnp.int32, (B, HD), 1)
@@ -75,14 +87,20 @@
     for b in range(B):
         length = jnp.where(row == b, lengths[b], length)
     usable = c * SEG + lane < length
+    my_length = lengths[mine]
     small[2].wait()
-    angle = length.astype(F32) * fbuf[...]
-    cosine = jnp.cos(angle)
-    sine = jnp.where(lane < HALF, -jnp.sin(angle), jnp.sin(angle))
+
+    def angles(positions):
+        angle = positions.astype(F32) * fbuf[...]
+        sine = jnp.sin(angle)
+        return jnp.cos(angle), jnp.where(lane < HALF, -sine, sine)
+
+    cosine, sine = angles(length)
+    my_cosine, my_sine = angles(jnp.full((B, HD), my_length, jnp.int32))
     small[0].wait()
     small[1].wait()
     stream = hbuf[...].astype(F32)
-    pl.semaphore_wait(barrier, 13)
+    pl.semaphore_wait(barrier, 22)
 
     def exchange(l, phase, width, peers):
         copies = []
@@ -133,28 +151,85 @@
             result.append(joined)
         return result, top, whole
 
+
+    def widen(l):
+        loads[l][3].wait()
+        loads[l][4].wait()
+        for b in range(B):
+            stage[l - 1, b, 0] = kbuf[l, b].astype(F32)
+            stage[l - 1, b, 1] = vbuf[l, b].astype(F32)
+        moved[l - 1, mine, 0] = stage[l - 1, mine, 0]
+        moved[l - 1, mine, 1] = stage[l - 1, mine, 1]
+
+    def move(l, unit):
+        which, rows = unit // (SEG // UNIT), pl.ds(unit % (SEG // UNIT) * UNIT, UNIT)
+        for d in (1, 4, 2, 6, 3, 5, 7):
+            to = lax.rem(mine + d, 8)
+            pltpu.make_async_remote_copy(
+                src_ref=stage.at[l - 1, to, which, rows],
+                dst_ref=moved.at[l - 1, mine, which, rows],
+                send_sem=bssem.at[l - 1, d - 1],
+                recv_sem=brsem.at[l - 1, d - 1],
+                device_id=(part * 8 + to, t),
+                device_id_type=MESH,
+            ).start()
+
+    def moves(l):
+        result = []
+        for d in range(1, 8):
+            origin = lax.rem(mine + 8 - d, 8)
+            result.append(
+                pltpu.make_async_remote_copy(
+                    src_ref=stage.at[l - 1, lax.rem(mine + d, 8)],
+                    dst_ref=moved.at[l - 1, origin],
+                    send_sem=bssem.at[l - 1, d - 1],
+                    recv_sem=brsem.at[l - 1, d - 1],
+                    device_id=(part * 8 + lax.rem(mine + d, 8), t),
+                    device_id_type=MESH,
+                )
+            )
+        return result
+
+    def narrow(l):
+        arrive(moves(l))
+        for s in range(8):
+            keys_t[l, :, s * SEG : (s + 1) * SEG] = moved[l - 1, s, 0].T.astype(BF16)
+            values[l - 1, s * SEG : (s + 1) * SEG] = moved[l - 1, s, 1].astype(BF16)
+
+    queue = [(l, u) for l in range(1, LAYERS) for u in range(2 * SEG // UNIT)]
+
+    def background():
+        for _ in range(min(PLAN[len(steps)], len(queue))):
+            l, u = queue.pop(0)
+            if u == 0:
+                widen(l)
+            move(l, u)
+        steps.append(1)
+
+    steps = []
     sent = []
-    for l in range(LAYERS):
-        load = loads[l]
-        gain = gbuf[l : l + 1, :].astype(F32)
-        scaled = (stream * gain).astype(BF16)
-        squares = stream * stream
-        squares = (tile(squares, 0) + tile(squares, 1)) + (tile(squares, 2) + tile(squares, 3))
-        for i in range(3):
-            load[i].wait()
+
+    within = part * 1024 + lax.broadcasted_iota(jnp.int32, (B, 1024), 1) < my_length
+
+    def first_layer(l, load, scaled, squares):
+        nonlocal sent
         snd[l, 0, :, :QA] = jnp.dot(scaled, wqkv[l, :, :QA], preferred_element_type=F32)
         snd[l, 0, :, QA : QA + HD] = squares
         a1 = exchange(l, 0, QA + HD, along_x)
         snd[l, 1, :, :QB] = jnp.dot(scaled, wqkv[l, :, QA:], preferred_element_type=F32)
         b1 = exchange(l, 1, QB, along_y)
+        load[3].wait()
+        load[4].wait()
+        for b in range(B):
+            keys_t[0, :, b * SEG : (b + 1) * SEG] = kbuf[0, b].astype(F32).T.astype(BF16)
+        background()
         arrive(a1)
         snd[l, 2, :, : QA + HD] = total(l, 0, QA + HD)
         a2 = exchange(l, 2, QA + HD, along_y)
         arrive(b1)
         snd[l, 3, :, :QB] = total(l, 1, QB)
         b2 = exchange(l, 3, QB, along_x)
-        load[3].wait()
-        load[4].wait()
+        background()
         arrive(a2)
         first = total(l, 2, QA + HD)
         inverse = lax.rsqrt(jnp.sum(tile(first, 5), axis=1, keepdims=True) / D + EPS)
@@ -170,8 +245,7 @@
         new_key = rotate(tile(second, 3)).astype(BF16).astype(F32)
         new_value = (tile(second, 4) * inverse).astype(BF16).astype(F32)
 
-        keys = kbuf[l].reshape(B * SEG, HD)
-        score = lax.dot_general(query, keys, (((1,), (1,)), ((), ())), preferred_element_type=F32)
+        score = jnp.dot(query, keys_t[l], preferred_element_type=F32)
         probs, tops, sums = [], [], []
         for h in range(8):
             block = score[h * B : (h + 1) * B]
@@ -200,6 +274,7 @@
         a3 = exchange(l, 4, 5 * HD, along_x)
         store_half(5, 4)
         b3 = exchange(l, 5, 5 * HD, along_y)
+        background()
         own = [jnp.zeros((B, HD), F32), jnp.zeros((B, HD), F32)]
         for h in range(8):
             dot = jnp.sum(query[h * B : (h + 1) * B].astype(F32) * new_key, axis=1, keepdims=True)
@@ -217,6 +292,7 @@
         arrive(b3)
         pass_on(5, 7)
         b4 = exchange(l, 7, 5 * HD, along_x)
+        background()
         load[5].wait()
         arrive(a4)
         context = jnp.concatenate(merge(l, 6, (own[0], new_value))[0], axis=1).astype(BF16)
@@ -224,6 +300,105 @@
         arrive(b4)
         context = jnp.concatenate(merge(l, 7, (own[1], new_value))[0], axis=1).astype(BF16)
         head_part = head_part + jnp.dot(context, wo[l, 4 * HD :, :], preferred_element_type=F32)
+        sent += a1 + b1 + a2 + b2 + a3 + b3 + a4 + b4
+        return head_part
+
+    def later_layer(l, load, scaled, squares):
+        nonlocal sent
+
+        raw = jnp.dot(scaled, wqkv[l], preferred_element_type=F32)
+        for i in range(10):
+            qsnd[l - 1, pl.ds(i, B, stride=16), :] = tile(raw, i)
+        qsnd[l - 1, pl.ds(10, B, stride=16), :] = squares
+        copies = []
+        for d in PLANE_ORDER:
+            to = plane[d - 1]
+            rows = pl.ds(pl.multiple_of(lax.rem(to[0], 8) * 16, 16), 11)
+            copy = pltpu.make_async_remote_copy(
+                src_ref=qsnd.at[l - 1, rows],
+                dst_ref=qrcv.at[l - 1, d - 1, pl.ds(0, 11)],
+                send_sem=qssem.at[l - 1, d - 1],
+                recv_sem=qrsem.at[l - 1, d - 1],
+                device_id=to,
+                device_id_type=MESH,
+            )
+            copy.start()
+            copies.append(copy)
+        sent += copies
+        background()
+        narrow(l)
+        at = pl.multiple_of(mine * 16, 16)
+        heads = [qsnd[l - 1, pl.ds(at, 8), :]]
+        others = [qsnd[l - 1, pl.ds(at + 8, 3), :]]
+        arrive(copies)
+        for d in range(15):
+            heads.append(qrcv[l - 1, d, 0:8, :])
+            others.append(qrcv[l - 1, d, 8:11, :])
+        heads, others = add_up(heads), add_up(others)
+        inverse = lax.rsqrt(jnp.sum(others[2:3], axis=1, keepdims=True) / D + EPS)
+
+        def rotate(u, rows):
+            u = u * inverse
+            return u * my_cosine[:rows] + pltpu.roll(u, HALF, 1) * my_sine[:rows]
+
+        query = rotate(heads, 8).astype(BF16)
+        new_key = rotate(jnp.broadcast_to(others[0:1], (B, HD)), 8).astype(BF16).astype(F32)
+        new_value = (others[1:2] * inverse).astype(BF16).astype(F32)
+        scale = 1.0 / math.sqrt(HD)
+        score = jnp.dot(query, keys_t[l], preferred_element_type=F32)
+        own = jnp.sum(query.astype(F32) * new_key, axis=1, keepdims=True) * scale
+        own = jnp.where(part == 0, own, FILL)
+        score = jnp.where(within, score * scale, FILL)
+        top = jnp.maximum(jnp.max(score, axis=1, keepdims=True), own)
+        p = jnp.where(within, jnp.exp(score - top), 0.0)
+        fresh = jnp.where(part == 0, jnp.exp(own - top), 0.0)
+        weight = jnp.sum(p, axis=1, keepdims=True) + fresh
+        mixed = jnp.dot(p.astype(BF16), values[l - 1], preferred_element_type=F32)
+        mixed = mixed + fresh.astype(BF16).astype(F32) * new_value
+        stats = jnp.where(lane == row, top, 0.0) + jnp.where(lane == row + HALF, weight, 0.0)
+        base = pl.multiple_of(c * 16, 16)
+        orcv[l - 1, pl.ds(base, 8), :] = mixed
+        orcv[l - 1, pl.ds(base + 8, 1), :] = jnp.sum(stats, axis=0, keepdims=True)
+        copies = []
+        for d in PLANE_ORDER:
+            copy = pltpu.make_async_remote_copy(
+                src_ref=orcv.at[l - 1, pl.ds(base, 9)],
+                dst_ref=orcv.at[l - 1, pl.ds(base, 9)],
+                send_sem=ossem.at[l - 1, d - 1],
+                recv_sem=orsem.at[l - 1, d - 1],
+                device_id=plane[d - 1],
+                device_id_type=MESH,
+            )
+            copy.start()
+            copies.append(copy)
+        sent += copies
+        background()
+        load[5].wait()
+        arrive(copies)
+        low = orcv[l - 1, pl.ds(8, B, stride=16), :]
+        high = orcv[l - 1, pl.ds(128 + 8, B, stride=16), :]
+        top = jnp.maximum(low, high)
+        scales = [jnp.exp(low - top), jnp.exp(high - top)]
+        whole = scales[0] * pltpu.roll(low, HALF, 1) + scales[1] * pltpu.roll(high, HALF, 1)
+        scales = [s / whole for s in scales]
+        context = []
+        for h in range(8):
+            context.append(
+                jnp.broadcast_to(scales[0][:, h : h + 1], (B, HD)) * orcv[l - 1, pl.ds(h, B, stride=16), :]
+                + jnp.broadcast_to(scales[1][:, h : h + 1], (B, HD)) * orcv[l - 1, pl.ds(128 + h, B, stride=16), :]
+            )
+        context = jnp.concatenate(context, axis=1).astype(BF16)
+        return jnp.dot(context, wo[l], preferred_element_type=F32)
+
+    for l in range(LAYERS):
+        load = loads[l]
+        gain = gbuf[l : l + 1, :].astype(F32)
+        scaled = (stream * gain).astype(BF16)
+        squares = stream * stream
+        squares = (tile(squares, 0) + tile(squares, 1)) + (tile(squares, 2) + tile(squares, 3))
+        for i in range(3):
+            load[i].wait()
+        head_part = (first_layer if l == 0 else later_layer)(l, load, scaled, squares)
 
         tpb[l, t] = head_part
         copies = []
@@ -238,13 +413,13 @@
             )
             copy.start()
             copies.append(copy)
-        sent += a1 + b1 + a2 + b2 + a3 + b3 + a4 + b4 + copies
+        sent += copies
+        background()
         arrive(copies)
-        gathered = [tpb[l, i] for i in range(8)]
-        while len(gathered) > 1:
-            gathered = [gathered[i] + gathered[i + 1] for i in range(0, len(gathered), 2)]
-        stream = stream + gathered[0]
+        stream = stream + add_up([tpb[l, i] for i in range(8)])
     out[...] = stream
+    for l in range(1, LAYERS):
+        sent += moves(l)
     for copy in sent:
         copy.wait_send()
 
@@ -267,16 +442,28 @@
             pltpu.VMEM((LAYERS, B, SEG, HD), BF16),
             pltpu.VMEM((LAYERS, B, SEG, HD), BF16),
             pltpu.VMEM((B, HD), F32),
-            pltpu.VMEM((LAYERS, 8, B, PART), F32),
-            pltpu.VMEM((LAYERS, 8, 3, B, PART), F32),
+            pltpu.VMEM((1, 8, B, PART), F32),
+            pltpu.VMEM((1, 8, 3, B, PART), F32),
             pltpu.VMEM((LAYERS, 8, B, 512), F32),
+            pltpu.VMEM((LAYERS, HD, B * SEG), BF16),
+            pltpu.VMEM((LAYERS - 1, B, 2, SEG, HD), F32),
+            pltpu.VMEM((LAYERS - 1, B, 2, SEG, HD), F32),
+            pltpu.VMEM((LAYERS - 1, B * SEG, HD), BF16),
+            pltpu.VMEM((LAYERS - 1, B * 16, HD), F32),
+            pltpu.VMEM((LAYERS - 1, 15, 16, HD), F32),
+            pltpu.VMEM((LAYERS - 1, 16 * 16, HD), F32),
             pltpu.SemaphoreType.DMA((LAYERS, 6)),
             pltpu.SemaphoreType.DMA((3,)),
-            pltpu.SemaphoreType.DMA((1,)),
-            pltpu.SemaphoreType.DMA((LAYERS, 8, 3)),
-            pltpu.SemaphoreType.DMA((LAYERS, 8, 3)),
+            pltpu.SemaphoreType.DMA((1, 8, 3)),
+            pltpu.SemaphoreType.DMA((1, 8, 3)),
             pltpu.SemaphoreType.DMA((LAYERS, 7)),
             pltpu.SemaphoreType.DMA((LAYERS, 7)),
+            pltpu.SemaphoreType.DMA((LAYERS - 1, 7)),
+            pltpu.SemaphoreType.DMA((LAYERS - 1, 7)),
+            pltpu.SemaphoreType.DMA((LAYERS - 1, 15)),
+            pltpu.SemaphoreType.DMA((LAYERS - 1, 15)),
+            pltpu.SemaphoreType.DMA((LAYERS - 1, 15)),
+            pltpu.SemaphoreType.DMA((LAYERS - 1, 15)),
         ],
         compiler_params=pltpu.CompilerParams(
             collective_id=0, has_side_effects=True, vmem_limit_bytes=60 * 1024 * 1024

time: 94.2 us -> 82.6 us (0.88)
  Pallas kernels: 92.7 us -> 81.1 us
    pallas_call x1, Pallas kernels: 92.7 us -> 81.1 us  [on_device(): pl.pallas_call(kernel, out_shape=jax.ShapeDtypeStruct((B, 512), F32), in_...]
where the time goes in v2:
time: 82.6 us; the launch traced here: 82.4 us
  Pallas kernels  81.1 us (98%)
  local copies, waits for them, and re-layouts  1.32 us (2%)
    pallas_call x1, Pallas kernels, on_device(): pl.pallas_call(kernel, out_shape=jax.ShapeDtypeStruct((B, 512), F32), in_...  81.1 us

profile of v2, /device:TPU:1, one launch (start us, length us, event | category | flops | bytes accessed | tf_op | source)
XLA Modules:
  0.0 82.4 jit_solution(1424031264359974753)
XLA Ops:
  0.0 81.1 %shard_map.100 = f32[8,512]{1,0:T(8,128)} custom-call(bf16[8,512]{1,0:T(8,128)(2,1)} %hidden.1, bf16[4,512]{1,0:T(4,128)(2,1)} %gains.1, bf16[4,512,1024]{2,1,0:T(8,128)(2,1)} %w_query.1, bf16[4,512,128]{2,1,0:T(8,128)(2,1)} %w_key.1, bf16[4,512,128]{2,1,0:T(8,128)(2,1)} %w_value.1, bf16[4,1024,512]{2,1,0:T(8,128)(2,1)} %w_out.1, ...), custom_call_target="tpu_custom_call" | custom-call | tf_op jit(solution)/shard_map/pallas_call | solution.py:432
  81.1 1.3 %copy.12 = f32[8,512]{1,0:T(8,128)} copy(f32[8,512]{1,0:T(8,128)} %shard_map.100) | data formatting | bytes 32768

commit v3 on v2

--- a/solution.py
+++ b/solution.py
@@ -26,7 +26,12 @@
 PART = 6 * HD
 PLANE_ORDER = (10, 6, 9, 11, 14, 2, 8, 5, 7, 13, 15, 1, 3, 4, 12)
 UNIT = 32
-PLAN = (2, 1, 2, 1, 3, 3, 2, 2, 2, 2, 2, 2, 0, 0)
+SHIFTS = ((1, 0), (2, 0), (3, 0), (0, 1), (1, 1), (2, 1), (3, 1))
+NEAR, FAR = (1, 3, 0, 2), (5, 4, 6)
+PLAN = (
+    (2, 2, 2, 2, 3, 2, 2, 3, 2, 2, 2, 0, 0, 0),
+    (0, 0, 3, 3, 3, 3, 2, 3, 2, 2, 3, 0, 0, 0),
+)
 
 
 def tile(value, i):
@@ -49,7 +54,18 @@
     c = lax.axis_index("ctx")
     t = lax.axis_index("tp")
     y, x = c // 4, lax.rem(c, 4)
-    mine, part = lax.rem(c, 8), c // 8
+    core = lax.rem(t, 2)
+
+    def seat(y, x):
+        u, v = x + core * (y - x), y + core * (x - y)
+        return v // 2, lax.rem(v, 2) * 4 + u
+
+    def place(part, sequence):
+        u, v = lax.rem(sequence, 4), part * 2 + sequence // 4
+        return (v + core * (u - v)) * 4 + u + core * (v - u)
+
+    part, mine = seat(y, x)
+    seat_index = part * 8 + mine
 
     def weight_loads(l):
         return (
@@ -66,20 +82,18 @@
         pltpu.make_async_copy(gains, gbuf, psem.at[1]),
         pltpu.make_async_copy(freq, fbuf, psem.at[2]),
     )
-    for copy in small:
-        copy.start()
-    loads = [weight_loads(l) for l in range(LAYERS)]
-    for group in loads:
-        for copy in group:
-            copy.start()
-
     along_x = [(y * 4 + lax.rem(x + d, 4), t) for d in (1, 2, 3)]
     along_y = [(lax.rem(y + d, 4) * 4 + x, t) for d in (1, 2, 3)]
     along_t = [(c, lax.rem(t + d, 8)) for d in range(1, 8)]
     plane = [(lax.rem(y + d // 4, 4) * 4 + lax.rem(x + d % 4, 4), t) for d in range(1, 16)]
     barrier = pltpu.get_barrier_semaphore()
-    for peer in plane + along_t:
+    for peer in along_x + along_y + along_t:
         pl.semaphore_signal(barrier, inc=1, device_id=peer, device_id_type=MESH)
+    for copy in small:
+        copy.start()
+    loads = [weight_loads(l) for l in range(LAYERS)]
+    for copy in loads[0][:3]:
+        copy.start()
 
     lane = lax.broadcasted_iota(jnp.int32, (B, HD), 1)
     row = lax.broadcasted_iota(jnp.int32, (B, HD), 0)
@@ -100,7 +114,6 @@
     small[0].wait()
     small[1].wait()
     stream = hbuf[...].astype(F32)
-    pl.semaphore_wait(barrier, 22)
 
     def exchange(l, phase, width, peers):
         copies = []
@@ -161,63 +174,79 @@
         moved[l - 1, mine, 0] = stage[l - 1, mine, 0]
         moved[l - 1, mine, 1] = stage[l - 1, mine, 1]
 
-    def move(l, unit):
+    def shifted(dx, other, sign=1):
+        return lax.rem(mine // 4 + other, 2) * 4 + lax.rem(lax.rem(mine, 4) + 4 + sign * dx, 4)
+
+    def moved_copy(l, j, to, src, dst):
+        return pltpu.make_async_remote_copy(
+            src_ref=src,
+            dst_ref=dst,
+            send_sem=bssem.at[l - 1, j],
+            recv_sem=brsem.at[l - 1, j],
+            device_id=(place(part, to), t),
+            device_id_type=MESH,
+        )
+
+    def move(l, unit, group):
         which, rows = unit // (SEG // UNIT), pl.ds(unit % (SEG // UNIT) * UNIT, UNIT)
-        for d in (1, 4, 2, 6, 3, 5, 7):
-            to = lax.rem(mine + d, 8)
-            pltpu.make_async_remote_copy(
-                src_ref=stage.at[l - 1, to, which, rows],
-                dst_ref=moved.at[l - 1, mine, which, rows],
-                send_sem=bssem.at[l - 1, d - 1],
-                recv_sem=brsem.at[l - 1, d - 1],
-                device_id=(part * 8 + to, t),
-                device_id_type=MESH,
+        for j in group:
+            to = shifted(*SHIFTS[j])
+            moved_copy(
+                l, j, to, stage.at[l - 1, to, which, rows], moved.at[l - 1, mine, which, rows]
             ).start()
 
     def moves(l):
         result = []
-        for d in range(1, 8):
-            origin = lax.rem(mine + 8 - d, 8)
-            result.append(
-                pltpu.make_async_remote_copy(
-                    src_ref=stage.at[l - 1, lax.rem(mine + d, 8)],
-                    dst_ref=moved.at[l - 1, origin],
-                    send_sem=bssem.at[l - 1, d - 1],
-                    recv_sem=brsem.at[l - 1, d - 1],
-                    device_id=(part * 8 + lax.rem(mine + d, 8), t),
-                    device_id_type=MESH,
-                )
-            )
+        for j in range(7):
+            to, origin = shifted(*SHIFTS[j]), shifted(*SHIFTS[j], sign=-1)
+            result.append(moved_copy(l, j, to, stage.at[l - 1, to], moved.at[l - 1, origin]))
         return result
 
     def narrow(l):
+        for queue, group in ((near, NEAR), (far, FAR)):
+            units(queue, sum(item[0] <= l for item in queue), group)
         arrive(moves(l))
         for s in range(8):
             keys_t[l, :, s * SEG : (s + 1) * SEG] = moved[l - 1, s, 0].T.astype(BF16)
             values[l - 1, s * SEG : (s + 1) * SEG] = moved[l - 1, s, 1].astype(BF16)
 
-    queue = [(l, u) for l in range(1, LAYERS) for u in range(2 * SEG // UNIT)]
+    widened = []
+
+    def units(queue, count, group):
+        for _ in range(min(count, len(queue))):
+            l, u = queue.pop(0)
+            if l not in widened:
+                widened.append(l)
+                widen(l)
+            move(l, u, group)
+
+    every = [(l, u) for l in range(1, LAYERS) for u in range(2 * SEG // UNIT)]
+    near, far = list(every), list(every)
 
     def background():
-        for _ in range(min(PLAN[len(steps)], len(queue))):
-            l, u = queue.pop(0)
-            if u == 0:
-                widen(l)
-            move(l, u)
+        units(near, PLAN[0][len(steps)], NEAR)
+        units(far, PLAN[1][len(steps)], FAR)
         steps.append(1)
 
     steps = []
     sent = []
 
-    within = part * 1024 + lax.broadcasted_iota(jnp.int32, (B, 1024), 1) < my_length
+    held = jnp.concatenate([place(part, s) * SEG + lane for s in range(B)], axis=1)
+    within = held < my_length
 
     def first_layer(l, load, scaled, squares):
         nonlocal sent
         snd[l, 0, :, :QA] = jnp.dot(scaled, wqkv[l, :, :QA], preferred_element_type=F32)
         snd[l, 0, :, QA : QA + HD] = squares
+        snd[l, 1, :, :QB] = jnp.dot(scaled, wqkv[l, :, QA:], preferred_element_type=F32)
+        pl.semaphore_wait(barrier, 13)
         a1 = exchange(l, 0, QA + HD, along_x)
-        snd[l, 1, :, :QB] = jnp.dot(scaled, wqkv[l, :, QA:], preferred_element_type=F32)
         b1 = exchange(l, 1, QB, along_y)
+        for copy in loads[0][3:]:
+            copy.start()
+        for group in loads[1:]:
+            for copy in group:
+                copy.start()
         load[3].wait()
         load[4].wait()
         for b in range(B):
@@ -313,7 +342,7 @@
         copies = []
         for d in PLANE_ORDER:
             to = plane[d - 1]
-            rows = pl.ds(pl.multiple_of(lax.rem(to[0], 8) * 16, 16), 11)
+            rows = pl.ds(pl.multiple_of(seat(to[0] // 4, lax.rem(to[0], 4))[1] * 16, 16), 11)
             copy = pltpu.make_async_remote_copy(
                 src_ref=qsnd.at[l - 1, rows],
                 dst_ref=qrcv.at[l - 1, d - 1, pl.ds(0, 11)],
@@ -356,7 +385,7 @@
         mixed = jnp.dot(p.astype(BF16), values[l - 1], preferred_element_type=F32)
         mixed = mixed + fresh.astype(BF16).astype(F32) * new_value
         stats = jnp.where(lane == row, top, 0.0) + jnp.where(lane == row + HALF, weight, 0.0)
-        base = pl.multiple_of(c * 16, 16)
+        base = pl.multiple_of(seat_index * 16, 16)
         orcv[l - 1, pl.ds(base, 8), :] = mixed
         orcv[l - 1, pl.ds(base + 8, 1), :] = jnp.sum(stats, axis=0, keepdims=True)
         copies = []

time: 82.6 us -> 77.7 us (0.941)
  Pallas kernels: 81.1 us -> 76.1 us
    pallas_call x1, Pallas kernels: 81.1 us -> 76.1 us  [on_device(): pl.pallas_call(kernel, out_shape=jax.ShapeDtypeStruct((B, 512), F32), in_...]
where the time goes in v3:
time: 77.7 us; the launch traced here: 77.5 us
  Pallas kernels  76.1 us (98%)
  local copies, waits for them, and re-layouts  1.32 us (2%)
    pallas_call x1, Pallas kernels, on_device(): pl.pallas_call(kernel, out_shape=jax.ShapeDtypeStruct((B, 512), F32), in_...  76.1 us

profile of v3, /device:TPU:1, one launch (start us, length us, event | category | flops | bytes accessed | tf_op | source)
XLA Modules:
  0.0 77.5 jit_solution(11652544303012289231)
XLA Ops:
  0.0 76.1 %shard_map.100 = f32[8,512]{1,0:T(8,128)} custom-call(bf16[8,512]{1,0:T(8,128)(2,1)} %hidden.1, bf16[4,512]{1,0:T(4,128)(2,1)} %gains.1, bf16[4,512,1024]{2,1,0:T(8,128)(2,1)} %w_query.1, bf16[4,512,128]{2,1,0:T(8,128)(2,1)} %w_key.1, bf16[4,512,128]{2,1,0:T(8,128)(2,1)} %w_value.1, bf16[4,1024,512]{2,1,0:T(8,128)(2,1)} %w_out.1, ...), custom_call_target="tpu_custom_call" | custom-call | tf_op jit(solution)/shard_map/pallas_call | solution.py:461
  76.1 1.3 %copy.12 = f32[8,512]{1,0:T(8,128)} copy(f32[8,512]{1,0:T(8,128)} %shard_map.100) | data formatting | bytes 32768

commit v4 on v3

--- a/solution.py
+++ b/solution.py
@@ -29,8 +29,8 @@
 SHIFTS = ((1, 0), (2, 0), (3, 0), (0, 1), (1, 1), (2, 1), (3, 1))
 NEAR, FAR = (1, 3, 0, 2), (5, 4, 6)
 PLAN = (
-    (2, 2, 2, 2, 3, 2, 2, 3, 2, 2, 2, 0, 0, 0),
-    (0, 0, 3, 3, 3, 3, 2, 3, 2, 2, 3, 0, 0, 0),
+    (2, 1, 2, 2, 3, 3, 3, 3, 2, 2, 1, 0, 0, 0),
+    (0, 0, 2, 3, 4, 3, 3, 3, 2, 2, 2, 0, 0, 0),
 )
 
 
@@ -46,9 +46,9 @@
 
 
 def kernel(
-    hidden, gains, w_query, w_key, w_value, w_out, key_cache, value_cache, lengths, freq,
+    hidden, gains, w_query, w_key, w_value, w_out, key_cache, value_cache, lengths_in, freq,
     out,
-    hbuf, gbuf, wqkv, wo, kbuf, vbuf, fbuf, snd, rcv, tpb, keys_t, stage, moved, values, qsnd, qrcv, orcv,
+    hbuf, gbuf, wqkv, wo, kbuf, vbuf, fbuf, snd, rcv, tpb, keys_t, stage, moved, values, qsnd, qrcv, orcv, obuf, lengths,
     lsem, psem, ssem, rsem, tssem, trsem, bssem, brsem, qssem, qrsem, ossem, orsem,
 ):
     c = lax.axis_index("ctx")
@@ -81,6 +81,7 @@
         pltpu.make_async_copy(hidden, hbuf, psem.at[0]),
         pltpu.make_async_copy(gains, gbuf, psem.at[1]),
         pltpu.make_async_copy(freq, fbuf, psem.at[2]),
+        pltpu.make_async_copy(lengths_in, lengths, psem.at[3]),
     )
     along_x = [(y * 4 + lax.rem(x + d, 4), t) for d in (1, 2, 3)]
     along_y = [(lax.rem(y + d, 4) * 4 + x, t) for d in (1, 2, 3)]
@@ -97,20 +98,26 @@
 
     lane = lax.broadcasted_iota(jnp.int32, (B, HD), 1)
     row = lax.broadcasted_iota(jnp.int32, (B, HD), 0)
-    length = jnp.zeros((B, HD), jnp.int32)
-    for b in range(B):
-        length = jnp.where(row == b, lengths[b], length)
-    usable = c * SEG + lane < length
-    my_length = lengths[mine]
-    small[2].wait()
-
-    def angles(positions):
-        angle = positions.astype(F32) * fbuf[...]
-        sine = jnp.sin(angle)
-        return jnp.cos(angle), jnp.where(lane < HALF, -sine, sine)
-
-    cosine, sine = angles(length)
-    my_cosine, my_sine = angles(jnp.full((B, HD), my_length, jnp.int32))
+    def positions():
+        small[3].wait()
+        length = jnp.zeros((B, HD), jnp.int32)
+        for b in range(B):
+            length = jnp.where(row == b, lengths[b], length)
+        usable = c * SEG + lane < length
+        my_length = lengths[mine]
+        small[2].wait()
+
+        def angles(positions):
+            angle = positions.astype(F32) * fbuf[...]
+            sine = jnp.sin(angle)
+            return jnp.cos(angle), jnp.where(lane < HALF, -sine, sine)
+
+        cosine, sine = angles(length)
+        my_cosine, my_sine = angles(jnp.full((B, HD), my_length, jnp.int32))
+        held = jnp.concatenate([place(part, s) * SEG + lane for s in range(B)], axis=1)
+        within = held < my_length
+        return usable, cosine, sine, my_cosine, my_sine, within
+
     small[0].wait()
     small[1].wait()
     stream = hbuf[...].astype(F32)
@@ -229,10 +236,8 @@
         steps.append(1)
 
     steps = []
+    shared = []
     sent = []
-
-    held = jnp.concatenate([place(part, s) * SEG + lane for s in range(B)], axis=1)
-    within = held < my_length
 
     def first_layer(l, load, scaled, squares):
         nonlocal sent
@@ -247,6 +252,8 @@
         for group in loads[1:]:
             for copy in group:
                 copy.start()
+        usable, cosine, sine, my_cosine, my_sine, within = known = positions()
+        shared.extend(known[3:])
         load[3].wait()
         load[4].wait()
         for b in range(B):
@@ -335,6 +342,7 @@
     def later_layer(l, load, scaled, squares):
         nonlocal sent
 
+        my_cosine, my_sine, within = shared
         raw = jnp.dot(scaled, wqkv[l], preferred_element_type=F32)
         for i in range(10):
             qsnd[l - 1, pl.ds(i, B, stride=16), :] = tile(raw, i)
@@ -446,11 +454,14 @@
         background()
         arrive(copies)
         stream = stream + add_up([tpb[l, i] for i in range(8)])
-    out[...] = stream
+    obuf[...] = stream
+    result = pltpu.make_async_copy(obuf, out, psem.at[0])
+    result.start()
     for l in range(1, LAYERS):
         sent += moves(l)
     for copy in sent:
         copy.wait_send()
+    result.wait()
 
 
 def on_device(hidden, norm_gains, w_query, w_key, w_value, w_out, key_cache, value_cache, lengths):
@@ -461,8 +472,8 @@
     return pl.pallas_call(
         kernel,
         out_shape=jax.ShapeDtypeStruct((B, 512), F32),
-        in_specs=[hbm] * 8 + [pl.BlockSpec(memory_space=pltpu.SMEM), hbm],
-        out_specs=pl.BlockSpec(memory_space=pltpu.VMEM),
+        in_specs=[hbm] * 10,
+        out_specs=hbm,
         scratch_shapes=[
             pltpu.VMEM((B, 512), BF16),
             pltpu.VMEM((LAYERS, 512), BF16),
@@ -481,8 +492,10 @@
             pltpu.VMEM((LAYERS - 1, B * 16, HD), F32),
             pltpu.VMEM((LAYERS - 1, 15, 16, HD), F32),
             pltpu.VMEM((LAYERS - 1, 16 * 16, HD), F32),
+            pltpu.VMEM((B, 512), F32),
+            pltpu.SMEM((B,), jnp.int32),
             pltpu.SemaphoreType.DMA((LAYERS, 6)),
-            pltpu.SemaphoreType.DMA((3,)),
+            pltpu.SemaphoreType.DMA((4,)),
             pltpu.SemaphoreType.DMA((1, 8, 3)),
             pltpu.SemaphoreType.DMA((1, 8, 3)),
             pltpu.SemaphoreType.DMA((LAYERS, 7)),

time: 77.7 us -> 76.7 us (0.987)
  Pallas kernels: 76.1 us -> 75.1 us
    pallas_call x1, Pallas kernels: 76.1 us -> 75.1 us  [on_device(): pl.pallas_call(kernel, out_shape=jax.ShapeDtypeStruct((B, 512), F32), in_...]
where the time goes in v4:
time: 76.7 us; the launch traced here: 76.4 us
  Pallas kernels  75.1 us (98%)
  local copies, waits for them, and re-layouts  1.32 us (2%)
    pallas_call x1, Pallas kernels, on_device(): pl.pallas_call(kernel, out_shape=jax.ShapeDtypeStruct((B, 512), F32), in_...  75.1 us

profile of v4, /device:TPU:1, one launch (start us, length us, event | category | flops | bytes accessed | tf_op | source)
XLA Modules:
  0.0 76.4 jit_solution(13126191934830893105)
XLA Ops:
  0.0 75.1 %shard_map.100 = f32[8,512]{1,0:T(8,128)} custom-call(bf16[8,512]{1,0:T(8,128)(2,1)} %hidden.1, bf16[4,512]{1,0:T(4,128)(2,1)} %gains.1, bf16[4,512,1024]{2,1,0:T(8,128)(2,1)} %w_query.1, bf16[4,512,128]{2,1,0:T(8,128)(2,1)} %w_key.1, bf16[4,512,128]{2,1,0:T(8,128)(2,1)} %w_value.1, bf16[4,1024,512]{2,1,0:T(8,128)(2,1)} %w_out.1, ...), custom_call_target="tpu_custom_call" | custom-call | tf_op jit(solution)/shard_map/pallas_call | solution.py:472
  75.1 1.3 %copy.12 = f32[8,512]{1,0:T(8,128)} copy(f32[8,512]{1,0:T(8,128)} %shard_map.100) | data formatting | bytes 32768

commit v5 on v4

--- a/solution.py
+++ b/solution.py
@@ -27,10 +27,10 @@
 PLANE_ORDER = (10, 6, 9, 11, 14, 2, 8, 5, 7, 13, 15, 1, 3, 4, 12)
 UNIT = 32
 SHIFTS = ((1, 0), (2, 0), (3, 0), (0, 1), (1, 1), (2, 1), (3, 1))
-NEAR, FAR = (1, 3, 0, 2), (5, 4, 6)
+NEAR, FAR = (0, 2, 3, 1), (4, 6, 5)
 PLAN = (
-    (2, 1, 2, 2, 3, 3, 3, 3, 2, 2, 1, 0, 0, 0),
-    (0, 0, 2, 3, 4, 3, 3, 3, 2, 2, 2, 0, 0, 0),
+    (1, 1, 1, 1, 4, 2, 2, 4, 2, 2, 4, 0, 0, 0),
+    (0, 0, 2, 2, 4, 2, 2, 4, 2, 2, 4, 0, 0, 0),
 )
 
 

time: 76.7 us -> 75.2 us (0.980)
  Pallas kernels: 75.1 us -> 73.6 us
    pallas_call x1, Pallas kernels: 75.1 us -> 73.6 us  [on_device(): pl.pallas_call(kernel, out_shape=jax.ShapeDtypeStruct((B, 512), F32), in_...]
where the time goes in v5:
time: 75.2 us; the launch traced here: 75 us
  Pallas kernels  73.6 us (98%)
  local copies, waits for them, and re-layouts  1.32 us (2%)
    pallas_call x1, Pallas kernels, on_device(): pl.pallas_call(kernel, out_shape=jax.ShapeDtypeStruct((B, 512), F32), in_...  73.6 us

profile of v5, /device:TPU:1, one launch (start us, length us, event | category | flops | bytes accessed | tf_op | source)
XLA Modules:
  0.0 75.0 jit_solution(4380218057289222168)
XLA Ops:
  0.0 73.6 %shard_map.100 = f32[8,512]{1,0:T(8,128)} custom-call(bf16[8,512]{1,0:T(8,128)(2,1)} %hidden.1, bf16[4,512]{1,0:T(4,128)(2,1)} %gains.1, bf16[4,512,1024]{2,1,0:T(8,128)(2,1)} %w_query.1, bf16[4,512,128]{2,1,0:T(8,128)(2,1)} %w_key.1, bf16[4,512,128]{2,1,0:T(8,128)(2,1)} %w_value.1, bf16[4,1024,512]{2,1,0:T(8,128)(2,1)} %w_out.1, ...), custom_call_target="tpu_custom_call" | custom-call | tf_op jit(solution)/shard_map/pallas_call | solution.py:472
  73.6 1.3 %copy.12 = f32[8,512]{1,0:T(8,128)} copy(f32[8,512]{1,0:T(8,128)} %shard_map.100) | data formatting | bytes 32768
